TPU v7x, 32 devices: a whole 2x2x4 slice. The times are simulated.
32 devices in a mesh: dp: 8 (over y, x, core), tensor: 4 (over z).
Axes of the slice: x: 2, y: 2, z: 4, core: 2. Of those that a mesh axis runs over, the one named last changes fastest.
Arguments:
- tokens_in: bfloat16 [8192, 1024], P(('dp', 'tensor')), may hold values from -6 to 6
- starts: int32 [8, 4], P('dp'), may hold values from 0 to 768, as said below
- ln1_gain: float32 [1024], P(('dp', 'tensor')), may hold values from 0.25 to 1.75
- ln1_bias: float32 [1024], P(('dp', 'tensor')), may hold values from -4 to 4
- w_qkv: bfloat16 [1024, 3072], P('dp', 'tensor'), may hold values from -0.25 to 0.25
- b_qv: bfloat16 [128, 16], P('tensor', 'dp'), may hold values from -6 to 6
- w_out: bfloat16 [1024, 1024], P('tensor', 'dp'), may hold values from -0.75 to 0.75
- b_out: float32 [1024], P(('dp', 'tensor')), may hold values from -6 to 6
- ln2_gain: float32 [1024], P(('dp', 'tensor')), may hold values from 0.25 to 1.75
- ln2_bias: float32 [1024], P(('dp', 'tensor')), may hold values from -4 to 4
- w_up: bfloat16 [1024, 4096], P('dp', 'tensor'), may hold values from -0.1875 to 0.1875
- b_up: bfloat16 [256, 16], P('tensor', 'dp'), may hold values from -6 to 6
- w_down: bfloat16 [4096, 1024], P('tensor', 'dp'), may hold values from -0.09375 to 0.09375
- b_down: float32 [1024], P(('dp', 'tensor')), may hold values from -6 to 6
- grad_out: bfloat16 [8192, 1024], P(('dp', 'tensor')), may hold values from -6 to 6
Outputs:
- output: bfloat16 [8192, 1024], P(('dp', 'tensor'))
- grad_tokens: bfloat16 [8192, 1024], P(('dp', 'tensor'))
- grad_ln1_gain: float32 [1024], P(('dp', 'tensor'))
- grad_ln1_bias: float32 [1024], P(('dp', 'tensor'))
- grad_w_qkv: float32 [1024, 3072], P('dp', 'tensor')
- grad_b_qv: float32 [128, 16], P('tensor', 'dp')
- grad_w_out: float32 [1024, 1024], P('tensor', 'dp')
- grad_b_out: float32 [1024], P(('dp', 'tensor'))
- grad_ln2_gain: float32 [1024], P(('dp', 'tensor'))
- grad_ln2_bias: float32 [1024], P(('dp', 'tensor'))
- grad_w_up: float32 [1024, 4096], P('dp', 'tensor')
- grad_b_up: float32 [256, 16], P('tensor', 'dp')
- grad_w_down: float32 [4096, 1024], P('tensor', 'dp')
- grad_b_down: float32 [1024], P(('dp', 'tensor'))
Inputs may be any that keep to these rules, and one draw needn't show every extreme that they name: starts[s, p] lies in the p-th of 4 equal regions of the sequence, and the span of 256 tokens from it ends inside that region.
All inputs are finite; a program needn't handle non-finite values.
Results may differ from a plain program's by a relative error of at most 0.02.
Values may be sent and summed in bfloat16 or wider, within the bound.
A program may use at most 128 MiB of HBM per device.

v0:
```python
import jax
import jax.numpy as jnp
from jax import lax
from jax.sharding import PartitionSpec as P

HD = 64
PIECE = 256
QBLOCK = 512
EPS = 1e-05
ROOT = 0.7978845608028654


def gelu_tanh(values):
    return 0.5 * values * (1.0 + jnp.tanh(ROOT * (values + 0.044715 * values * values * values)))


def normalize(values):
    center = jnp.mean(values, axis=-1, keepdims=True)
    shifted = values - center
    inverse = lax.rsqrt(jnp.mean(shifted * shifted, axis=-1, keepdims=True) + EPS)
    return (shifted * inverse, inverse)


def norm_back(grad_normed, normed, inverse, gain):
    scaled = grad_normed * gain
    return inverse * (
        scaled
        - jnp.mean(scaled, axis=-1, keepdims=True)
        - normed * jnp.mean(scaled * normed, axis=-1, keepdims=True)
    )


def dot_last(left, right):
    return lax.dot_general(
        left, right, (((1,), (1,)), ((), ())), preferred_element_type=jnp.float32
    )


def dot_first(left, right):
    return lax.dot_general(
        left, right, (((0,), (0,)), ((), ())), preferred_element_type=jnp.float32
    )


def gather_rows(values):
    return lax.all_gather(values, "tensor", axis=0, tiled=True)


def gather_grads(values):
    return lax.all_gather(values, "tensor", axis=0, tiled=True)


def reduce_rows(left, weight, rows):

    def term(start, count):
        return jnp.dot(left, weight, preferred_element_type=jnp.float32)

    return lax.psum_scatter(
        term(jnp.int32(0), lax.axis_size("tensor") * rows).astype(jnp.bfloat16),
        "tensor",
        scatter_dimension=0,
        tiled=True,
    ).astype(jnp.float32)


def reduce_grads(left, weight, rows):

    def term(start, count):
        return dot_last(left, weight)

    return lax.psum_scatter(
        term(jnp.int32(0), lax.axis_size("tensor") * rows).astype(jnp.bfloat16),
        "tensor",
        scatter_dimension=0,
        tiled=True,
    ).astype(jnp.float32)


def piece_ids(start_row, length):
    places = jnp.arange(length, dtype=jnp.int32)
    inside = (places[:, None] >= start_row[None, :]) & (
        places[:, None] < start_row[None, :] + PIECE
    )
    labels = jnp.arange(1, start_row.shape[0] + 1, dtype=jnp.int32)
    return jnp.sum(jnp.where(inside, labels[None, :], 0), axis=1)


def allowed_block(row_ids, row_places, key_ids, key_places):
    causal = key_places[None, :] <= row_places[:, None]
    picture = (row_ids[:, None] == key_ids[None, :]) & (row_ids[:, None] > 0)
    return causal | picture


def block_scores(by_seq, start_rows, block_index):
    length = by_seq.shape[1]
    per_seq = length // QBLOCK
    seq_index = block_index // per_seq
    first_row = block_index % per_seq * QBLOCK
    sequence = lax.dynamic_index_in_dim(by_seq, seq_index, 0, keepdims=False)
    key_ids = piece_ids(lax.dynamic_index_in_dim(start_rows, seq_index, 0, keepdims=False), length)
    query_rows = lax.dynamic_slice_in_dim(sequence, first_row, QBLOCK, 0)[:, :, 0]
    key_rows = sequence[:, :, 1]
    value_rows = sequence[:, :, 2]
    row_ids = lax.dynamic_slice_in_dim(key_ids, first_row, QBLOCK, 0)
    row_places = first_row + jnp.arange(QBLOCK, dtype=jnp.int32)
    scores = (
        jnp.einsum("qhd,khd->hqk", query_rows, key_rows, preferred_element_type=jnp.float32) * 0.125
    )
    places = jnp.arange(length, dtype=jnp.int32)
    scores = jnp.where(allowed_block(row_ids, row_places, key_ids, places)[None], scores, -1e30)
    return (seq_index, first_row, query_rows, key_rows, value_rows, scores)


def attention_forward(by_seq, start_rows):
    total_blocks = by_seq.shape[0] * (by_seq.shape[1] // QBLOCK)

    def attend(block_index):
        _, _, query_rows, key_rows, value_rows, scores = block_scores(
            by_seq, start_rows, block_index
        )
        peak = jnp.max(scores, axis=-1, keepdims=True)
        log_total = peak + jnp.log(jnp.sum(jnp.exp(scores - peak), axis=-1, keepdims=True))
        probs = jnp.exp(scores - log_total)
        heads = jnp.einsum(
            "hqk,khd->qhd",
            probs.astype(jnp.bfloat16),
            value_rows,
            preferred_element_type=jnp.float32,
        )
        return (heads.astype(jnp.bfloat16), log_total)

    return lax.map(attend, jnp.arange(total_blocks, dtype=jnp.int32))


def attention_backward(by_seq, start_rows, log_totals, grad_heads):
    total_blocks = by_seq.shape[0] * (by_seq.shape[1] // QBLOCK)
    empty = jnp.zeros(by_seq.shape[:3] + (HD,), jnp.float32)

    def step(carry, item):
        grad_keys, grad_values = carry
        block_index, log_total = item
        seq_index, first_row, query_rows, key_rows, value_rows, scores = block_scores(
            by_seq, start_rows, block_index
        )
        grad_seq = lax.dynamic_index_in_dim(grad_heads, seq_index, 0, keepdims=False)
        grad_rows = lax.dynamic_slice_in_dim(grad_seq, first_row, QBLOCK, 0)
        probs = jnp.exp(scores - log_total)
        grad_probs = jnp.einsum(
            "qhd,khd->hqk", grad_rows, value_rows, preferred_element_type=jnp.float32
        )
        inner = jnp.sum(probs * grad_probs, axis=-1, keepdims=True)
        grad_scores = (probs * (grad_probs - inner)).astype(jnp.bfloat16)
        grad_query = (
            jnp.einsum("hqk,khd->qhd", grad_scores, key_rows, preferred_element_type=jnp.float32)
            * 0.125
        )
        key_term = (
            jnp.einsum("hqk,qhd->khd", grad_scores, query_rows, preferred_element_type=jnp.float32)
            * 0.125
        )
        value_term = jnp.einsum(
            "hqk,qhd->khd",
            probs.astype(jnp.bfloat16),
            grad_rows,
            preferred_element_type=jnp.float32,
        )
        grad_keys = lax.dynamic_update_index_in_dim(
            grad_keys,
            lax.dynamic_index_in_dim(grad_keys, seq_index, 0, keepdims=False) + key_term,
            seq_index,
            0,
        )
        grad_values = lax.dynamic_update_index_in_dim(
            grad_values,
            lax.dynamic_index_in_dim(grad_values, seq_index, 0, keepdims=False) + value_term,
            seq_index,
            0,
        )
        return ((grad_keys, grad_values), grad_query)

    (grad_keys, grad_values), grad_query = lax.scan(
        step, (empty, empty), (jnp.arange(total_blocks, dtype=jnp.int32), log_totals)
    )
    return (grad_query, grad_keys, grad_values)


def per_device(
    tokens_in,
    starts,
    ln1_gain,
    ln1_bias,
    w_qkv,
    b_qv,
    w_out,
    b_out,
    ln2_gain,
    ln2_bias,
    w_up,
    b_up,
    w_down,
    b_down,
    grad_out,
):
    rows = tokens_in.shape[0]
    gain_one, shift_one, bias_out, gain_two, shift_two, bias_down = (
        lax.all_gather(ln1_gain, ("dp", "tensor"), axis=0, tiled=True),
        lax.all_gather(ln1_bias, ("dp", "tensor"), axis=0, tiled=True),
        lax.all_gather(b_out, ("dp", "tensor"), axis=0, tiled=True),
        lax.all_gather(ln2_gain, ("dp", "tensor"), axis=0, tiled=True),
        lax.all_gather(ln2_bias, ("dp", "tensor"), axis=0, tiled=True),
        lax.all_gather(b_down, ("dp", "tensor"), axis=0, tiled=True),
    )
    weight_qkv, bias_qv, weight_out = (
        lax.all_gather(w_qkv, "dp", axis=0, tiled=True),
        lax.all_gather(b_qv, "dp", axis=1, tiled=True),
        lax.all_gather(w_out, "dp", axis=1, tiled=True),
    )
    weight_up, bias_up, weight_down = (
        lax.all_gather(w_up, "dp", axis=0, tiled=True),
        lax.all_gather(b_up, "dp", axis=1, tiled=True),
        lax.all_gather(w_down, "dp", axis=1, tiled=True),
    )
    local_heads = weight_qkv.shape[1] // (3 * HD)
    seq_count = starts.shape[0]
    inputs = tokens_in.astype(jnp.float32)
    normed_one, inverse_one = normalize(inputs)
    gathered_one = gather_rows((normed_one * gain_one + shift_one).astype(jnp.bfloat16))
    group = gathered_one.shape[0]
    length = group // seq_count
    bias_pair = bias_qv.astype(jnp.float32).reshape(local_heads, 2, HD)
    full_bias = jnp.stack(
        [bias_pair[:, 0], jnp.zeros_like(bias_pair[:, 0]), bias_pair[:, 1]], axis=1
    )
    projected = (
        jnp.dot(gathered_one, weight_qkv, preferred_element_type=jnp.float32).reshape(
            group, local_heads, 3, HD
        )
        + full_bias
    ).astype(jnp.bfloat16)
    by_seq = projected.reshape(seq_count, length, local_heads, 3, HD)
    heads_blocks, log_totals = attention_forward(by_seq, starts)
    heads_out = heads_blocks.reshape(group, local_heads * HD)
    middle = inputs + (reduce_rows(heads_out, weight_out, rows) + bias_out)
    normed_two, inverse_two = normalize(middle)
    rounded_two = (normed_two * gain_two + shift_two).astype(jnp.bfloat16)
    grad_final = grad_out.astype(jnp.float32)
    grad_bias_down = jnp.sum(grad_final, axis=0)
    gathered_two = gather_rows(rounded_two)
    up_proj = jnp.dot(gathered_two, weight_up, preferred_element_type=jnp.float32) + bias_up.astype(
        jnp.float32
    ).reshape(-1)
    hidden_act, gelu_pull = jax.vjp(gelu_tanh, up_proj)
    hidden_low = hidden_act.astype(jnp.bfloat16)
    output = (middle + reduce_rows(hidden_low, weight_down, rows) + bias_down).astype(jnp.bfloat16)
    grad_branch = gather_grads(grad_out)
    grad_w_down = dot_first(hidden_low, grad_branch)
    grad_up = gelu_pull(dot_last(grad_branch, weight_down))[0].astype(jnp.bfloat16)
    grad_b_up = jnp.sum(grad_up, axis=0, dtype=jnp.float32).reshape(bias_up.shape)
    grad_w_up = dot_first(gathered_two, grad_up)
    grad_two = reduce_grads(grad_up, weight_up, rows)
    grad_w_up, grad_b_up, grad_w_down = (
        lax.psum_scatter(
            grad_w_up.astype(jnp.bfloat16), "dp", scatter_dimension=0, tiled=True
        ).astype(jnp.float32),
        lax.psum_scatter(
            grad_b_up.astype(jnp.bfloat16), "dp", scatter_dimension=1, tiled=True
        ).astype(jnp.float32),
        lax.psum_scatter(
            grad_w_down.astype(jnp.bfloat16), "dp", scatter_dimension=1, tiled=True
        ).astype(jnp.float32),
    )
    grad_gain_two = jnp.sum(grad_two * normed_two, axis=0)
    grad_shift_two = jnp.sum(grad_two, axis=0)
    grad_middle = grad_final + norm_back(grad_two, normed_two, inverse_two, gain_two)
    grad_bias_out = jnp.sum(grad_middle, axis=0)
    grad_attn = gather_grads(grad_middle.astype(jnp.bfloat16))
    grad_w_out = dot_first(heads_out, grad_attn)
    grad_heads = (
        dot_last(grad_attn, weight_out)
        .astype(jnp.bfloat16)
        .reshape(seq_count, length, local_heads, HD)
    )
    grad_query, grad_keys, grad_values = attention_backward(by_seq, starts, log_totals, grad_heads)
    grad_proj = jnp.stack(
        [
            grad_query.reshape(group, local_heads, HD),
            grad_keys.reshape(group, local_heads, HD),
            grad_values.reshape(group, local_heads, HD),
        ],
        axis=2,
    ).astype(jnp.bfloat16)
    grad_b_qv = jnp.sum(grad_proj[:, :, 0::2], axis=0, dtype=jnp.float32).reshape(bias_qv.shape)
    grad_flat = grad_proj.reshape(group, 3 * local_heads * HD)
    grad_w_qkv = dot_first(gathered_one, grad_flat)
    grad_one = reduce_grads(grad_flat, weight_qkv, rows)
    grad_w_qkv, grad_b_qv, grad_w_out = (
        lax.psum_scatter(
            grad_w_qkv.astype(jnp.bfloat16), "dp", scatter_dimension=0, tiled=True
        ).astype(jnp.float32),
        lax.psum_scatter(
            grad_b_qv.astype(jnp.bfloat16), "dp", scatter_dimension=1, tiled=True
        ).astype(jnp.float32),
        lax.psum_scatter(
            grad_w_out.astype(jnp.bfloat16), "dp", scatter_dimension=1, tiled=True
        ).astype(jnp.float32),
    )
    grad_gain_one = jnp.sum(grad_one * normed_one, axis=0)
    grad_shift_one = jnp.sum(grad_one, axis=0)
    grad_tokens = (grad_middle + norm_back(grad_one, normed_one, inverse_one, gain_one)).astype(
        jnp.bfloat16
    )
    summed = (
        lax.psum_scatter(grad_gain_one, ("dp", "tensor"), scatter_dimension=0, tiled=True),
        lax.psum_scatter(grad_shift_one, ("dp", "tensor"), scatter_dimension=0, tiled=True),
        lax.psum_scatter(grad_bias_out, ("dp", "tensor"), scatter_dimension=0, tiled=True),
        lax.psum_scatter(grad_gain_two, ("dp", "tensor"), scatter_dimension=0, tiled=True),
        lax.psum_scatter(grad_shift_two, ("dp", "tensor"), scatter_dimension=0, tiled=True),
        lax.psum_scatter(grad_bias_down, ("dp", "tensor"), scatter_dimension=0, tiled=True),
    )
    return (
        output,
        grad_tokens,
        summed[0],
        summed[1],
        grad_w_qkv,
        grad_b_qv,
        grad_w_out,
        summed[2],
        summed[3],
        summed[4],
        grad_w_up,
        grad_b_up,
        grad_w_down,
        summed[5],
    )


def solution(mesh):
    return jax.shard_map(
        per_device,
        mesh=mesh,
        in_specs=(
            P(("dp", "tensor"), None),
            P("dp", None),
            P(("dp", "tensor")),
            P(("dp", "tensor")),
            P("dp", "tensor"),
            P("tensor", "dp"),
            P("tensor", "dp"),
            P(("dp", "tensor")),
            P(("dp", "tensor")),
            P(("dp", "tensor")),
            P("dp", "tensor"),
            P("tensor", "dp"),
            P("tensor", "dp"),
            P(("dp", "tensor")),
            P(("dp", "tensor"), None),
        ),
        out_specs=(
            P(("dp", "tensor"), None),
            P(("dp", "tensor"), None),
            P(("dp", "tensor")),
            P(("dp", "tensor")),
            P("dp", "tensor"),
            P("tensor", "dp"),
            P("tensor", "dp"),
            P(("dp", "tensor")),
            P(("dp", "tensor")),
            P(("dp", "tensor")),
            P("dp", "tensor"),
            P("tensor", "dp"),
            P("tensor", "dp"),
            P(("dp", "tensor")),
        ),
        check_vma=False,
    )
```

profile of v0, /device:TPU:12, one launch (start us, length us, event | category | flops | bytes accessed | tf_op | source)
XLA Modules:
  0.0 705.2 jit_solution(5103127675943364345)
XLA Ops:
  12.2 41.6 %all-reduce.15 = (f32[1024]{0:T(1024)S(1)}, f32[1024]{0:T(1024)S(1)}, f32[1024]{0:T(1024)S(1)}, f32[1024]{0:T(1024)S(1)}, f32[1024]{0:T(1024)S(1)}) all-reduce(f32[1024]{0:T(1024)S(1)} %dynamic-update-slice.4, f32[1024]{0:T(1024)S(1)} %dynamic-update-slice.3, ...), channel_id=1, replica_groups=mesh['dp'=8,'tensor'=4] {'dp','tensor'}, use_global_device_ids=true, to_apply=%add.4 | all-reduce | flops 5120 | bytes 40960
  54.9 1.3 fusion.63
  56.3 2.1 fusion.58
  58.5 7.9 %all-gather = bf16[8,2,32]{2,1,0:T(2,128)(2,1)S(1)} all-gather(bf16[1,2,32]{2,1,0:T(2,128)(2,1)} %bitcast.220), channel_id=1, replica_groups=mesh['dp'=8,'tensor'=4] {'dp'}, dimensions={0}, use_global_device_ids=true | all-gather | bytes 1152 | tf_op jit(solution)/shard_map/all_gather | solution.py:215
  66.7 10.4 %all_gather.53 = bf16[256,1024]{1,0:T(8,128)(2,1)S(1)} all-gather(bf16[256,128]{1,0:T(8,128)(2,1)} %param.25), channel_id=1, replica_groups=mesh['dp'=8,'tensor'=4] {'dp'}, dimensions={1}, use_global_device_ids=true | all-gather | bytes 589824 | tf_op jit(solution)/shard_map/all_gather | solution.py:216
  77.1 24.8 %all-gather.10.cloned.1.call-done = bf16[1024,1024]{1,0:T(8,128)(2,1)} async-done(((bf16[256,1024]{1,0:T(8,128)(2,1)}), bf16[1024,1024]{1,0:T(8,128)(2,1)}) %all-gather.10.cloned.1.call-update) | async-done | bytes 2097168 | tf_op jit(solution)/shard_map/all_gather | solution.py:46
  101.9 3.9 fusion.75
  106.5 19.6 %while.30 = (s32[]{:T(128)}, bf16[2,512,4,64]{1,3,2,0:T(8,128)(2,1)S(1)}, f32[2,4,512,1]{2,1,3,0:T(4,128)S(1)}, s32[2]{0:T(128)S(1)}, s32[1,4]{1,0:T(1,128)S(1)}...) while((s32[]{:T(128)}, ...), condition=%wide.region_6.7_spmd, body=%wide.region_2.6_spmd.sunk | while | flops 562186240 | bytes 30494096 | solution.py:132
  110.0 1.7 fusion.114
  111.7 2.3 exponential_reduce_fusion.2
  114.0 2.2 fusion.115
  119.8 1.7 fusion.114
  121.5 2.3 exponential_reduce_fusion.2
  123.8 2.2 fusion.115
  127.5 2.2 convolution_convert_fusion.4
  130.4 42.5 %reduce-scatter.15.cloned.1.call-done = bf16[256,1024]{1,0:T(8,128)(2,1)} async-done(((bf16[1024,1024]{1,0:T(8,128)(2,1)}), bf16[256,1024]{1,0:T(8,128)(2,1)}) %reduce-scatter.15.cloned.1.call-update) | async-done | bytes 524304 | tf_op jit(solution)/shard_map/reduce_scatter | solution.py:58
  174.1 1.4 multiply_reduce_fusion.1
  175.5 2.1 add_convert_fusion.1
  179.1 9.0 %all-gather.1 = bf16[8,2,64]{2,1,0:T(2,128)(2,1)S(1)} all-gather(bf16[1,2,64]{2,1,0:T(2,128)(2,1)S(1)} %bitcast.221), channel_id=1, replica_groups=mesh['dp'=8,'tensor'=4] {'dp'}, dimensions={0}, use_global_device_ids=true | all-gather | bytes 2304 | tf_op jit(solution)/shard_map/all_gather | solution.py:220
  188.2 14.1 %all-gather.16.cloned.1.call-done = bf16[1024,1024]{1,0:T(8,128)(2,1)} async-done(((bf16[128,1024]{1,0:T(8,128)(2,1)}), bf16[1024,1024]{1,0:T(8,128)(2,1)}) %all-gather.16.cloned.1.call-update) | async-done | bytes 2097168 | tf_op jit(solution)/shard_map/all_gather | solution.py:219
  202.4 46.4 %all-gather.14.cloned.1.call-done = bf16[1024,1024]{1,0:T(8,128)(2,1)} async-done(((bf16[256,1024]{1,0:T(8,128)(2,1)}), bf16[1024,1024]{1,0:T(8,128)(2,1)}) %all-gather.14.cloned.1.call-update) | async-done | bytes 2097168 | tf_op jit(solution)/shard_map/all_gather | solution.py:46
  248.8 6.5 fusion.76
  255.3 39.4 %all-gather.20.cloned.1.call-done = bf16[1024,1024]{1,0:T(8,128)(2,1)} async-done(((bf16[256,1024]{1,0:T(8,128)(2,1)}), bf16[1024,1024]{1,0:T(8,128)(2,1)}) %all-gather.20.cloned.1.call-update) | async-done | bytes 2097168 | tf_op jit(solution)/shard_map/all_gather | solution.py:50
  294.7 29.8 %all-gather.18.cloned.1.call-done = bf16[1024,1024]{1,0:T(8,128)(2,1)} async-done(((bf16[1024,128]{1,0:T(8,128)(2,1)}), bf16[1024,1024]{1,0:T(8,128)(2,1)}) %all-gather.18.cloned.1.call-update) | async-done | bytes 2097168 | tf_op jit(solution)/shard_map/all_gather | solution.py:221
  324.5 9.6 %fusion.71 = (bf16[1024]{0:T(1024)(128)(2,1)}, bf16[1024,1024]{1,0:T(8,128)(2,1)S(1)}) fusion(f32[1024,1024]{1,0:T(8,128)} %fusion.76, f32[1024]{0:T(1024)S(1)} %reshape.318, bf16[1024,1024]{1,0:T(8,128)(2,1)} %all-gather.20.cloned.1.call-done, bf16[1024,1024]{1,0:T(8,128)(2,1)} %all-gather.18.cloned.1.call-done), kind=kOutput, calls=%fused_computation.142 | convolution fusion | flops 2174745600 | bytes 10491904 | tf_op jit(solution)/shard_map/dot_general | solution.py:34
  334.1 1.3 copy-done.26
  335.4 3.7 convolution_convert_fusion.2
  339.2 43.2 %reduce-scatter.19.cloned.1.call-done = bf16[256,1024]{1,0:T(8,128)(2,1)} async-done(((bf16[1024,1024]{1,0:T(8,128)(2,1)}), bf16[256,1024]{1,0:T(8,128)(2,1)}) %reduce-scatter.19.cloned.1.call-update) | async-done | bytes 524304 | tf_op jit(solution)/shard_map/reduce_scatter | solution.py:71
  382.4 1.7 fusion.68
  384.1 1.7 fusion.73
  387.9 7.2 %convolution_convert_fusion = bf16[1024,1024]{1,0:T(8,128)(2,1)} fusion(bf16[1024,1024]{1,0:T(8,128)(2,1)} %all-gather.20.cloned.1.call-done, f32[1024,1024]{1,0:T(8,128)} %fusion.76, f32[1024]{0:T(1024)S(1)} %reshape.318), kind=kOutput, calls=%fused_computation.82 | convolution fusion | flops 2159017984 | bytes 8392704 | tf_op jit(solution)/shard_map/dot_general | solution.py:40
  395.2 4.0 copy.63
  399.3 6.0 convolution_convert_fusion.1
  405.3 26.9 %all-gather.22.cloned.1.call-done = bf16[1024,1024]{1,0:T(8,128)(2,1)} async-done(((bf16[256,1024]{1,0:T(8,128)(2,1)}), bf16[1024,1024]{1,0:T(8,128)(2,1)}) %all-gather.22.cloned.1.call-update) | async-done | bytes 2097168 | tf_op jit(solution)/shard_map/all_gather | solution.py:50
  432.2 3.1 convolution_convert_fusion.7
  435.3 2.0 copy.60
  437.8 3.1 convolution_convert_fusion.8
  442.2 56.8 %while.31 = (s32[]{:T(128)}, f32[1,1024,4,64]{1,3,2,0:T(8,128)S(1)}, f32[1,1024,4,64]{1,3,2,0:T(8,128)}, bf16[2,512,4,64]{1,0,3,2:T(2,128)(2,1)}, s32[2]{0:T(128...) while((s32[]{:T(128)}, ...), condition=%wide.region_17.18_spmd, body=%wide.region_14.17_spmd.sunk | while | flops 1376798720 | bytes 76885448 | solution.py:181
  447.0 4.5 fusion.123
  451.5 3.2 multiply_reduce_fusion.3
  454.7 2.4 multiply_convert_fusion.5
  457.0 1.4 fusion.124
  460.6 9.9 %dynamic_update_slice.31 = bf16[2,512,4,64]{1,0,3,2:T(2,128)(2,1)} dynamic-update-slice(bf16[2,512,4,64]{1,0,3,2:T(2,128)(2,1)} %get-tuple-element.503, bf16[1,512,4,64]{1,0,3,2:T(2,128)(2,1)} %copy.86, s32[]{:T(128)S(6)} %copy.108, s32[]{:T(128)} %constant.208.clone.1..sunk.1, s32[]{:T(128)} %constant.208.clone.1..sunk.1, s32[]{:T(128)} %constant.208.clone.1..sunk.1) | dynamic-update-slice | bytes 524292 | tf_op jit(solution)/shard_map/while/body/jit(dynamic_update_index_in_dim)/dynamic_update_slice | solution.py:181
  475.3 4.5 fusion.123
  479.8 3.2 multiply_reduce_fusion.3
  482.9 2.4 multiply_convert_fusion.5
  485.3 1.4 fusion.124
  488.9 9.9 %dynamic_update_slice.31 = bf16[2,512,4,64]{1,0,3,2:T(2,128)(2,1)} dynamic-update-slice(bf16[2,512,4,64]{1,0,3,2:T(2,128)(2,1)} %get-tuple-element.503, bf16[1,512,4,64]{1,0,3,2:T(2,128)(2,1)} %copy.86, s32[]{:T(128)S(6)} %copy.108, s32[]{:T(128)} %constant.208.clone.1..sunk.1, s32[]{:T(128)} %constant.208.clone.1..sunk.1, s32[]{:T(128)} %constant.208.clone.1..sunk.1) | dynamic-update-slice | bytes 524292 | tf_op jit(solution)/shard_map/while/body/jit(dynamic_update_index_in_dim)/dynamic_update_slice | solution.py:181
  499.0 2.2 stack_reshape.9
  501.2 1.8 maximum_convert_fusion
  503.2 1.3 copy-done.12
  504.5 3.0 convolution_convert_fusion.6
  507.6 5.1 convolution_convert_fusion.5
  512.8 7.1 %convolution_convert_fusion.3 = bf16[1024,1024]{1,0:T(8,128)(2,1)} fusion(bf16[1024,1024]{1,0:T(8,128)(2,1)} %all-gather.18.cloned.1.call-done, f32[1024,1024]{1,0:T(8,128)} %fusion.76, f32[1024]{0:T(1024)S(1)} %reshape.318), kind=kOutput, calls=%fused_computation.85 | convolution fusion | flops 2159017984 | bytes 8392704 | tf_op jit(solution)/shard_map/dot_general | solution.py:56
  523.5 1.8 convert_element_type.168
  525.3 1.4 slice_reduce_fusion
  526.8 22.9 %all-reduce.16 = (bf16[32,16]{1,0:T(8,128)(2,1)S(1)}, bf16[64,16]{1,0:T(8,128)(2,1)S(1)}) all-reduce(bf16[32,16]{1,0:T(8,128)(2,1)S(1)} %convert_element_type.163, bf16[64,16]{1,0:T(8,128)(2,1)S(1)} %convert_element_type.169), channel_id=9, replica_groups=mesh['dp'=8,'tensor'=4] {'dp'}, use_global_device_ids=true, to_apply=%region_27.28.clone | all-reduce | flops 1536 | bytes 6144
  551.2 7.5 %reduce-scatter.27.cloned.1.call-done = bf16[128,256]{1,0:T(8,128)(2,1)} async-done(((bf16[1024,256]{1,0:T(8,128)(2,1)}), bf16[128,256]{1,0:T(8,128)(2,1)}) %reduce-scatter.27.cloned.1.call-update) | async-done | bytes 65552
  560.3 40.0 %reduce-scatter.23.cloned.1.call-done = bf16[128,768]{1,0:T(8,128)(2,1)} async-done(((bf16[1024,768]{1,0:T(8,128)(2,1)}), bf16[128,768]{1,0:T(8,128)(2,1)}) %reduce-scatter.23.cloned.1.call-update) | async-done | bytes 196624 | tf_op jit(solution)/shard_map/reduce_scatter | solution.py:297
  600.4 1.7 convert_element_type.162
  602.1 43.3 %reduce-scatter.21.cloned.1.call-done = bf16[256,1024]{1,0:T(8,128)(2,1)} async-done(((bf16[1024,1024]{1,0:T(8,128)(2,1)}), bf16[256,1024]{1,0:T(8,128)(2,1)}) %reduce-scatter.21.cloned.1.call-update) | async-done | bytes 524304 | tf_op jit(solution)/shard_map/reduce_scatter | solution.py:71
  645.4 1.6 fusion.69
  647.0 45.3 %all-reduce.14 = (f32[1024]{0:T(1024)S(1)}, f32[1024]{0:T(1024)S(1)}, f32[1024]{0:T(1024)S(1)}, f32[1024]{0:T(1024)S(1)}, f32[1024]{0:T(1024)S(1)}, /*index=5*/f32[1024]{0:T(1024)S(1)}, f32[1024]{0:T(1024)S(1)}) all-reduce(f32[1024]{0:T(1024)S(1)} %dynamic-update-slice.5, ...), channel_id=1, replica_groups=mesh['dp'=8,'tensor'=4] {'dp','tensor'}, use_global_device_ids=true, to_apply=%add.5 | all-reduce | flops 7168 | bytes 57344
  695.8 2.7 fusion.62
  (185 shorter events, 38.8 us)
Async XLA Ops:
  7.2 70.0 %all-gather.12.cloned.1.call-start = ((), (), s32[]{:S(2)}) async-start(), calls=%async_computation.9 | async-start | bytes 1769472 | tf_op jit(solution)/shard_map/all_gather | solution.py:214
  7.9 94.0 %all-gather.10.cloned.1.call-start = ((), (), s32[]{:S(2)}) async-start(), calls=%async_computation.8 | async-start | bytes 2621440 | tf_op jit(solution)/shard_map/all_gather | solution.py:46
  53.7 4.7 copy-start.14
  54.9 3.5 copy-start.16
  56.3 2.2 copy-start.18
  58.5 114.4 %reduce-scatter.15.cloned.1.call-start = ((), (), s32[]{:S(2)}) async-start(), calls=%async_computation.10 | async-start | bytes 2621440 | tf_op jit(solution)/shard_map/reduce_scatter | solution.py:58
  77.1 49.6 %copy-start.8 = (bf16[256,1024]{1,0:T(8,128)(2,1)}, bf16[256,1024]{1,0:T(8,128)(2,1)S(1)}, u32[]{:S(2)}) copy-start(bf16[256,1024]{1,0:T(8,128)(2,1)S(1)} %all_gather.53) | copy-start | bytes 1572868
  105.8 0.7 copy-start.13
  126.1 46.7 %copy-start = (bf16[256,1024]{1,0:T(8,128)(2,1)S(1)}, bf16[256,1024]{1,0:T(8,128)(2,1)}, u32[]{:S(2)}) copy-start(bf16[256,1024]{1,0:T(8,128)(2,1)} %param.19) | copy-start | bytes 1572868
  126.7 0.8 copy-start.10
  129.7 49.4 %copy-start.21 = (bf16[64,2]{0,1:T(2,128)(2,1)S(1)}, bf16[64,2]{0,1:T(2,128)(2,1)}, u32[]{:S(2)}) copy-start(bf16[64,2]{0,1:T(2,128)(2,1)} %param.30) | copy-start | bytes 772
  129.7 72.6 %all-gather.16.cloned.1.call-start = ((), (), s32[]{:S(2)}) async-start(), calls=%async_computation.12 | async-start | bytes 2359296 | tf_op jit(solution)/shard_map/all_gather | solution.py:219
  130.3 118.5 %all-gather.14.cloned.1.call-start = ((), (), s32[]{:S(2)}) async-start(), calls=%async_computation.11 | async-start | bytes 2621440 | tf_op jit(solution)/shard_map/all_gather | solution.py:46
  177.7 117.0 %all-gather.20.cloned.1.call-start = ((), (), s32[]{:S(2)}) async-start(), calls=%async_computation.15 | async-start | bytes 2621440 | tf_op jit(solution)/shard_map/all_gather | solution.py:50
  178.3 146.2 %all-gather.18.cloned.1.call-start = ((), (), s32[]{:S(2)}) async-start(), calls=%async_computation.13 | async-start | bytes 2359296 | tf_op jit(solution)/shard_map/all_gather | solution.py:221
  179.0 203.4 %reduce-scatter.19.cloned.1.call-start = ((), (), s32[]{:S(2)}) async-start(), calls=%async_computation.16 | async-start | bytes 2621440 | tf_op jit(solution)/shard_map/reduce_scatter | solution.py:71
  324.5 10.9 %copy-start.23 = (bf16[1024,1024]{1,0:T(8,128)(2,1)S(1)}, bf16[1024,1024]{1,0:T(8,128)(2,1)}, u32[]{:S(2)}) copy-start(bf16[1024,1024]{1,0:T(8,128)(2,1)} %all-gather.16.cloned.1.call-done) | copy-start | bytes 6291460
  334.1 1.3 copy-start.26
  335.4 47.0 %copy-start.1 = (bf16[256,1024]{1,0:T(8,128)(2,1)S(1)}, bf16[256,1024]{1,0:T(8,128)(2,1)}, u32[]{:S(2)}) copy-start(bf16[256,1024]{1,0:T(8,128)(2,1)} %reduce-scatter.15.cloned.1.call-done) | copy-start | bytes 1572868
  335.4 48.7 %copy-start.7 = (bf16[256,1024]{1,0:T(8,128)(2,1)S(1)}, bf16[256,1024]{1,0:T(8,128)(2,1)}, u32[]{:S(2)}) copy-start(bf16[256,1024]{1,0:T(8,128)(2,1)} %param.33) | copy-start | bytes 1572868
  339.1 93.1 %all-gather.22.cloned.1.call-start = ((), (), s32[]{:S(2)}) async-start(), calls=%async_computation.17 | async-start | bytes 2621440 | tf_op jit(solution)/shard_map/all_gather | solution.py:50
  385.8 1.0 copy-start.4
  387.7 133.9 %reduce-scatter.29.cloned.1.call-start = ((), (), s32[]{:S(2)}) async-start(), calls=%async_computation.22 | async-start | bytes 2359296
  399.2 33.0 %copy-start.11 = (bf16[32,8,2,512]{3,1,2,0:T(8,128)(2,1)S(1)}, bf16[32,8,2,512]{3,1,2,0:T(8,128)(2,1)}, u32[]{:S(2)}) copy-start(bf16[32,8,2,512]{3,1,2,0:T(8,128)(2,1)} %copy-done.10) | copy-start | bytes 1572868
  399.2 124.3 %reduce-scatter.25.cloned.1.call-start = ((), (), s32[]{:S(2)}) async-start(), calls=%async_computation.20 | async-start | bytes 2359296 | tf_op jit(solution)/shard_map/reduce_scatter | solution.py:262
  405.3 32.6 %copy-start.9 = (bf16[256,1024]{1,0:T(8,128)(2,1)S(1)}, bf16[256,1024]{1,0:T(8,128)(2,1)}, u32[]{:S(2)}) copy-start(bf16[256,1024]{1,0:T(8,128)(2,1)} %copy-done.8) | copy-start | bytes 1572868
  405.3 153.4 %reduce-scatter.27.cloned.1.call-start = ((), (), s32[]{:S(2)}) async-start(), calls=%async_computation.21 | async-start | bytes 589824
  437.4 163.0 %reduce-scatter.23.cloned.1.call-start = ((), (), s32[]{:S(2)}) async-start(), calls=%async_computation.19 | async-start | bytes 1769472 | tf_op jit(solution)/shard_map/reduce_scatter | solution.py:297
  445.7 1.3 copy-start.6
  474.0 1.3 copy-start.6
  501.2 3.3 copy-start.22
  503.0 4.5 copy-start.3
  503.2 1.3 copy-start.12
  507.6 137.8 %reduce-scatter.21.cloned.1.call-start = ((), (), s32[]{:S(2)}) async-start(), calls=%async_computation.18 | async-start | bytes 2621440 | tf_op jit(solution)/shard_map/reduce_scatter | solution.py:71
  512.7 7.2 %copy-start.25 = (u32[32]{0:T(128)S(1)}, u32[32]{0:T(128)}, u32[]{:S(2)}) copy-start(u32[32]{0:T(128)} %constant.252) | copy-start | bytes 388
  512.7 8.5 %copy-start.24 = (f32[32]{0:T(128)S(1)}, f32[32]{0:T(128)}, u32[]{:S(2)}) copy-start(f32[32]{0:T(128)} %param.32) | copy-start | bytes 388
  512.8 8.7 %copy-start.20 = (bf16[1024]{0:T(1024)(128)(2,1)S(1)}, bf16[1024]{0:T(1024)(128)(2,1)}, u32[]{:S(2)}) copy-start(bf16[1024]{0:T(1024)(128)(2,1)} %get-tuple-element.314) | copy-start | bytes 6148
  512.8 183.0 %reduce-scatter.17.cloned.1.call-start = ((), (), s32[]{:S(2)}) async-start(), calls=%async_computation.14 | async-start | bytes 2621440 | tf_op jit(solution)/shard_map/reduce_scatter | solution.py:58
  519.9 125.5 %copy-start.15 = (f32[1024]{0:T(1024)S(1)}, f32[1024]{0:T(1024)}, u32[]{:S(2)}) copy-start(f32[1024]{0:T(1024)} %copy-done.14) | copy-start | bytes 12292
  519.9 125.5 %copy-start.17 = (f32[256]{0:T(256)S(1)}, f32[256]{0:T(256)}, u32[]{:S(2)}) copy-start(f32[256]{0:T(256)} %copy-done.16) | copy-start | bytes 3076
  519.9 125.5 %copy-start.19 = (f32[256]{0:T(256)S(1)}, f32[256]{0:T(256)}, u32[]{:S(2)}) copy-start(f32[256]{0:T(256)} %copy-done.18) | copy-start | bytes 3076
  519.9 175.9 %copy-start.2 = (bf16[256,1024]{1,0:T(8,128)(2,1)S(1)}, bf16[256,1024]{1,0:T(8,128)(2,1)}, u32[]{:S(2)}) copy-start(bf16[256,1024]{1,0:T(8,128)(2,1)} %reduce-scatter.15.cloned.1.call-done) | copy-start | bytes 1572868
  519.9 175.9 %copy-start.5 = (f32[256,1024]{1,0:T(8,128)S(1)}, f32[256,1024]{1,0:T(8,128)}, u32[]{:S(2)}) copy-start(f32[256,1024]{1,0:T(8,128)} %copy-done.4) | copy-start | bytes 3145732
Sparse Core Ops, SparseCore 0:
  9.9 26.7 all-gather.11
  58.5 43.3 all-gather.9
  129.8 42.9 reduce-scatter.14
  174.6 27.7 all-gather.15
  204.3 44.4 all-gather.13
  250.2 44.4 all-gather.19
  296.6 27.8 all-gather.17
  339.2 43.1 reduce-scatter.18
  387.8 44.3 all-gather.21
  435.3 41.1 reduce-scatter.28
  479.9 41.1 reduce-scatter.24
  524.5 34.1 reduce-scatter.26
  562.0 38.3 reduce-scatter.22
  602.5 42.8 reduce-scatter.20
  647.5 43.8 reduce-scatter.16
where the time goes:
time: 711 us; the launch traced here: 705 us
  waiting for transfers between devices  361 us (51%)
  blocking collectives  137 us (19%)
  matrix products  91 us (13%)
  local copies, waits for them, and re-layouts  52.4 us (7%)
  other arithmetic  39.5 us (6%)
  between operations  15.2 us (2%)
  loops' own time  8.27 us (1%)
    unnamed x3, blocking collectives  110 us
    reduce_scatter x2, waiting for transfers between devices, reduce_grads(): lax.psum_scatter(term(jnp.int32(0), lax.axis_size('tensor') * rows).astyp...  86.5 us
    all_gather x2, waiting for transfers between devices, gather_rows(): return lax.all_gather(values, 'tensor', axis=0, tiled=True)  71.2 us
    all_gather x2, waiting for transfers between devices, gather_grads(): return lax.all_gather(values, 'tensor', axis=0, tiled=True)  66.2 us
    reduce_scatter x2, waiting for transfers between devices, reduce_rows(): lax.psum_scatter(term(jnp.int32(0), lax.axis_size('tensor') * rows).astyp...  42.5 us
    reduce_scatter x1, waiting for transfers between devices, per_device(): lax.psum_scatter(grad_w_qkv.astype(jnp.bfloat16), 'dp', scatter_dimension...  40 us
    all_gather x1, waiting for transfers between devices, per_device(): lax.all_gather(w_down, 'dp', axis=1, tiled=True)  29.8 us
    unnamed x78, local copies, waits for them, and re-layouts  22.9 us
  transfers between devices with their start and end apart: 15, of which 11 were waited for; matrix products, arithmetic and copies ran while one was open for 19% of the time, Pallas kernels for 0%

commit v1 on v0

--- a/solution.py
+++ b/solution.py
@@ -8,6 +8,13 @@
 QBLOCK = 512
 EPS = 1e-05
 ROOT = 0.7978845608028654
+
+
+def plan_the_forms(local_x, join_dim):
+    h_now = list(local_x.shape[1:])
+    h_now[join_dim] *= local_x.shape[0]
+    work_now = jnp.moveaxis(local_x, 0, join_dim).reshape(h_now)
+    return work_now
 
 
 def gelu_tanh(values):
@@ -47,7 +54,30 @@
 
 
 def gather_grads(values):
-    return lax.all_gather(values, "tensor", axis=0, tiled=True)
+
+    def write_knots_on_mesh(row_data, across, on_dim):
+        n_all = lax.axis_size(across)
+        opened = range(n_all)
+        parts_out = map(lambda s: (s, (s + 1) % n_all), opened)
+        line_up = list(parts_out)
+        samples = [(at, d) for d, at in line_up]
+        side_arr, y = ([], [])
+        for q in range(n_all - 1):
+            if q % 2 == 0:
+                r2 = lax.ppermute(side_arr[-1] if side_arr else row_data, across, line_up)
+                side_arr.append(r2)
+            else:
+                m_next = lax.ppermute(y[-1] if y else row_data, across, samples)
+                y.append(m_next)
+        item_now = jnp.stack([*side_arr[::-1], row_data, *y], axis=0)
+        w_next = lax.axis_index(across)
+        outer = len(side_arr)
+        block_out = w_next - outer
+        item_now = item_now[(jnp.arange(n_all) - block_out) % n_all]
+        met_up = plan_the_forms(item_now, on_dim)
+        return met_up
+
+    return write_knots_on_mesh(values, "tensor", 0)
 
 
 def reduce_rows(left, weight, rows):

time: 711 us -> 616 us (0.87)
  waiting for transfers between devices: 361 us -> 242 us
  starting transfers between devices: 1.22 us -> 11.5 us
  local copies, waits for them, and re-layouts: 52.4 us -> 59.6 us
    all_gather x2 -> x0, waiting for transfers between devices: 66.2 us -> none  [gather_grads(): return lax.all_gather(values, 'tensor', axis=0, tiled=True)]
    ppermute x0 -> x6, waiting for transfers between devices: none -> 52.3 us  [the longest x4 52.3 us: write_knots_on_mesh(): r2 = lax.ppermute(side_arr[-1] if side_arr else row_data, across, line_up)]
    reduce_scatter x1, waiting for transfers between devices: 40 us -> 1.19 us  [per_device(): lax.psum_scatter(grad_w_qkv.astype(jnp.bfloat16), 'dp', scatter_dimension...]
    all_gather x2, waiting for transfers between devices: 71.2 us -> 51.3 us  [gather_rows(): return lax.all_gather(values, 'tensor', axis=0, tiled=True)]
    reduce_scatter x2, waiting for transfers between devices: 86.5 us -> 69.1 us  [reduce_grads(): lax.psum_scatter(term(jnp.int32(0), lax.axis_size('tensor') * rows).astyp...]
    all_gather x1, waiting for transfers between devices: 14.1 us -> 0.01 us  [per_device(): lax.all_gather(w_up, 'dp', axis=0, tiled=True)]
    ppermute x0 -> x6, starting transfers between devices: none -> 10.3 us  [the longest x4 9.33 us: write_knots_on_mesh(): r2 = lax.ppermute(side_arr[-1] if side_arr else row_data, across, line_up)]
    unnamed x17 -> x15, waiting for transfers between devices: 10.2 us -> 1.9 us
  transfers between devices with their start and end apart: 15 -> 19, of which waited for: 11 -> 11; matrix products, arithmetic and copies ran while one was open for 19% -> 25% of each run, Pallas kernels for 0% -> 0%
where the time goes in v1:
time: 616 us; the launch traced here: 609 us
  waiting for transfers between devices  242 us (39%)
  blocking collectives  135 us (22%)
  matrix products  90.9 us (15%)
  local copies, waits for them, and re-layouts  59.6 us (10%)
  other arithmetic  46.2 us (8%)
  between operations  15.2 us (2%)
  starting transfers between devices  11.5 us (2%)
  loops' own time  8.27 us (1%)
    unnamed x3, blocking collectives  108 us
    reduce_scatter x2, waiting for transfers between devices, reduce_grads(): lax.psum_scatter(term(jnp.int32(0), lax.axis_size('tensor') * rows).astyp...  69.1 us
    ppermute x4, waiting for transfers between devices, write_knots_on_mesh(): r2 = lax.ppermute(side_arr[-1] if side_arr else row_data, across, line_up)  52.3 us
    all_gather x2, waiting for transfers between devices, gather_rows(): return lax.all_gather(values, 'tensor', axis=0, tiled=True)  51.3 us
    reduce_scatter x2, waiting for transfers between devices, reduce_rows(): lax.psum_scatter(term(jnp.int32(0), lax.axis_size('tensor') * rows).astyp...  42.5 us
    all_gather x1, waiting for transfers between devices, per_device(): lax.all_gather(w_down, 'dp', axis=1, tiled=True)  23.6 us
    unnamed x74, local copies, waits for them, and re-layouts  22.9 us
    dynamic_update_slice x4, local copies, waits for them, and re-layouts, attention_backward(): lax.scan(step, (empty, empty), (jnp.arange(total_blocks, dtype=jnp.int32)...  22.2 us
  transfers between devices with their start and end apart: 19, of which 11 were waited for; matrix products, arithmetic and copies ran while one was open for 25% of the time, Pallas kernels for 0%

profile of v1, /device:TPU:12, one launch (start us, length us, event | category | flops | bytes accessed | tf_op | source)
XLA Modules:
  0.0 608.6 jit_solution(5609862049060437253)
XLA Ops:
  12.2 41.6 %all-reduce.15 = (f32[1024]{0:T(1024)S(1)}, f32[1024]{0:T(1024)S(1)}, f32[1024]{0:T(1024)S(1)}, f32[1024]{0:T(1024)S(1)}, f32[1024]{0:T(1024)S(1)}) all-reduce(f32[1024]{0:T(1024)S(1)} %dynamic-update-slice.4, f32[1024]{0:T(1024)S(1)} %dynamic-update-slice.3, ...), channel_id=1, replica_groups=mesh['dp'=8,'tensor'=4] {'dp','tensor'}, use_global_device_ids=true, to_apply=%add.4 | all-reduce | flops 5120 | bytes 40960
  56.3 2.1 fusion.58
  58.5 7.9 %all-gather = bf16[8,2,32]{2,1,0:T(2,128)(2,1)S(1)} all-gather(bf16[1,2,32]{2,1,0:T(2,128)(2,1)} %bitcast.238), channel_id=1, replica_groups=mesh['dp'=8,'tensor'=4] {'dp'}, dimensions={0}, use_global_device_ids=true | all-gather | bytes 1152 | tf_op jit(solution)/shard_map/all_gather | solution.py:245
  66.7 10.4 %all_gather.47 = bf16[256,1024]{1,0:T(8,128)(2,1)S(1)} all-gather(bf16[256,128]{1,0:T(8,128)(2,1)} %param.25), channel_id=1, replica_groups=mesh['dp'=8,'tensor'=4] {'dp'}, dimensions={1}, use_global_device_ids=true | all-gather | bytes 589824 | tf_op jit(solution)/shard_map/all_gather | solution.py:246
  77.1 24.8 %all-gather.8.cloned.1.call-done = bf16[1024,1024]{1,0:T(8,128)(2,1)} async-done(((bf16[256,1024]{1,0:T(8,128)(2,1)}), bf16[1024,1024]{1,0:T(8,128)(2,1)}) %all-gather.8.cloned.1.call-update) | async-done | bytes 2097168 | tf_op jit(solution)/shard_map/all_gather | solution.py:53
  101.9 3.9 fusion.77
  106.5 19.6 %while.30 = (s32[]{:T(128)}, bf16[2,512,4,64]{1,3,2,0:T(8,128)(2,1)S(1)}, f32[2,4,512,1]{2,1,3,0:T(4,128)S(1)}, s32[2]{0:T(128)S(1)}, s32[1,4]{1,0:T(1,128)S(1)}...) while((s32[]{:T(128)}, ...), condition=%wide.region_6.7_spmd, body=%wide.region_2.6_spmd.sunk | while | flops 562186240 | bytes 30494096 | solution.py:162
  110.0 1.7 fusion.116
  111.7 2.3 exponential_reduce_fusion.2
  114.0 2.2 fusion.117
  119.8 1.7 fusion.116
  121.5 2.3 exponential_reduce_fusion.2
  123.8 2.2 fusion.117
  127.5 2.1 convolution_convert_fusion.4
  130.3 42.5 %reduce-scatter.15.cloned.1.call-done = bf16[256,1024]{1,0:T(8,128)(2,1)} async-done(((bf16[1024,1024]{1,0:T(8,128)(2,1)}), bf16[256,1024]{1,0:T(8,128)(2,1)}) %reduce-scatter.15.cloned.1.call-update) | async-done | bytes 524304 | tf_op jit(solution)/shard_map/reduce_scatter | solution.py:88
  175.4 2.1 add_convert_fusion.1
  178.2 1.6 collective-permute-start
  180.3 21.5 %collective-permute-done = bf16[256,1024]{1,0:T(8,128)(2,1)} collective-permute-done((bf16[256,1024]{1,0:T(8,128)(2,1)S(1)}, bf16[256,1024]{1,0:T(8,128)(2,1)}, u32[]{:S(2)}, u32[]{:S(2)}) %collective-permute-start) | collective-permute-done | bytes 524320 | tf_op jit(solution)/shard_map/ppermute | solution.py:67
  201.8 3.1 collective-permute-start.1
  204.9 8.9 %all-gather.1 = bf16[8,2,64]{2,1,0:T(2,128)(2,1)S(1)} all-gather(bf16[1,2,64]{2,1,0:T(2,128)(2,1)S(1)} %bitcast.239), channel_id=1, replica_groups=mesh['dp'=8,'tensor'=4] {'dp'}, dimensions={0}, use_global_device_ids=true | all-gather | bytes 2304 | tf_op jit(solution)/shard_map/all_gather | solution.py:250
  214.0 1.7 collective-permute-done.1
  215.7 3.0 pad_maximum_fusion
  218.7 3.6 gather_fusion
  222.3 26.5 %all-gather.12.cloned.1.call-done = bf16[1024,1024]{1,0:T(8,128)(2,1)} async-done(((bf16[256,1024]{1,0:T(8,128)(2,1)}), bf16[1024,1024]{1,0:T(8,128)(2,1)}) %all-gather.12.cloned.1.call-update) | async-done | bytes 2097168 | tf_op jit(solution)/shard_map/all_gather | solution.py:53
  248.8 6.5 %fusion.78 = f32[1024,1024]{1,0:T(8,128)} fusion(bf16[1024,1024]{1,0:T(8,128)(2,1)} %all-gather.12.cloned.1.call-done, bf16[1024,1024]{1,0:T(8,128)(2,1)} %all-gather.14.cloned.1.call-done), kind=kOutput, calls=%fused_computation.157 | convolution fusion | flops 2147483648 | bytes 8388608 | tf_op jit(solution)/shard_map/dot_general | solution.py:279
  255.2 23.6 %all-gather.16.cloned.1.call-done = bf16[1024,1024]{1,0:T(8,128)(2,1)} async-done(((bf16[1024,128]{1,0:T(8,128)(2,1)}), bf16[1024,1024]{1,0:T(8,128)(2,1)}) %all-gather.16.cloned.1.call-update) | async-done | bytes 2097168 | tf_op jit(solution)/shard_map/all_gather | solution.py:251
  278.9 9.6 %fusion.73 = (bf16[1024]{0:T(1024)(128)(2,1)}, bf16[1024,1024]{1,0:T(8,128)(2,1)S(1)}) fusion(f32[1024,1024]{1,0:T(8,128)} %fusion.78, f32[1024]{0:T(1024)S(1)} %reshape.375, bf16[1024,1024]{1,0:T(8,128)(2,1)} %bitcast.219, bf16[1024,1024]{1,0:T(8,128)(2,1)} %all-gather.16.cloned.1.call-done), kind=kOutput, calls=%fused_computation.153 | convolution fusion | flops 2174745600 | bytes 10491904 | tf_op jit(solution)/shard_map/dot_general | solution.py:41
  289.8 3.7 convolution_convert_fusion.2
  293.8 7.2 %convolution_convert_fusion = bf16[1024,1024]{1,0:T(8,128)(2,1)} fusion(bf16[1024,1024]{1,0:T(8,128)(2,1)} %bitcast.220, f32[1024,1024]{1,0:T(8,128)} %fusion.78, f32[1024]{0:T(1024)S(1)} %reshape.375), kind=kOutput, calls=%fused_computation.86 | convolution fusion | flops 2159017984 | bytes 8392704 | tf_op jit(solution)/shard_map/dot_general | solution.py:47
  301.0 3.9 copy.63
  305.0 6.0 convolution_convert_fusion.1
  311.1 25.7 %reduce-scatter.19.cloned.1.call-done = bf16[256,1024]{1,0:T(8,128)(2,1)} async-done(((bf16[1024,1024]{1,0:T(8,128)(2,1)}), bf16[256,1024]{1,0:T(8,128)(2,1)}) %reduce-scatter.19.cloned.1.call-update) | async-done | bytes 524304 | tf_op jit(solution)/shard_map/reduce_scatter | solution.py:101
  336.8 1.7 fusion.68
  338.5 1.8 fusion.75
  341.5 1.6 collective-permute-start.3
  343.6 21.6 %collective-permute-done.3 = bf16[256,1024]{1,0:T(8,128)(2,1)} collective-permute-done((bf16[256,1024]{1,0:T(8,128)(2,1)S(1)}, bf16[256,1024]{1,0:T(8,128)(2,1)}, u32[]{:S(2)}, u32[]{:S(2)}) %collective-permute-start.3) | collective-permute-done | bytes 524320 | tf_op jit(solution)/shard_map/ppermute | solution.py:67
  365.2 3.1 collective-permute-start.4
  369.6 7.5 %collective-permute-done.4 = bf16[256,1024]{1,0:T(8,128)(2,1)} collective-permute-done((bf16[256,1024]{1,0:T(8,128)(2,1)}, bf16[256,1024]{1,0:T(8,128)(2,1)}, u32[]{:S(2)}, u32[]{:S(2)}) %collective-permute-start.4) | collective-permute-done | bytes 524320 | tf_op jit(solution)/shard_map/ppermute | solution.py:67
  377.1 3.0 pad_maximum_fusion.1
  380.1 3.7 gather_fusion.1
  383.8 3.1 convolution_convert_fusion.7
  386.9 2.0 copy.60
  388.9 3.2 convolution_convert_fusion.8
  393.8 56.8 %while.31 = (s32[]{:T(128)}, f32[1,1024,4,64]{1,3,2,0:T(8,128)S(1)}, f32[1,1024,4,64]{1,3,2,0:T(8,128)}, bf16[2,512,4,64]{1,0,3,2:T(2,128)(2,1)}, s32[2]{0:T(128...) while((s32[]{:T(128)}, ...), condition=%wide.region_17.18_spmd, body=%wide.region_14.17_spmd.sunk | while | flops 1376798720 | bytes 76885448 | solution.py:211
  398.6 4.5 fusion.125
  403.1 3.2 multiply_reduce_fusion.3
  406.3 2.4 multiply_convert_fusion.5
  412.2 9.9 %dynamic_update_slice.31 = bf16[2,512,4,64]{1,0,3,2:T(2,128)(2,1)} dynamic-update-slice(bf16[2,512,4,64]{1,0,3,2:T(2,128)(2,1)} %get-tuple-element.503, bf16[1,512,4,64]{1,0,3,2:T(2,128)(2,1)} %copy.86, s32[]{:T(128)S(6)} %copy.108, s32[]{:T(128)} %constant.230.clone.1..sunk.1, s32[]{:T(128)} %constant.230.clone.1..sunk.1, s32[]{:T(128)} %constant.230.clone.1..sunk.1) | dynamic-update-slice | bytes 524292 | tf_op jit(solution)/shard_map/while/body/jit(dynamic_update_index_in_dim)/dynamic_update_slice | solution.py:211
  426.9 4.5 fusion.125
  431.4 3.2 multiply_reduce_fusion.3
  434.6 2.4 multiply_convert_fusion.5
  440.5 9.9 %dynamic_update_slice.31 = bf16[2,512,4,64]{1,0,3,2:T(2,128)(2,1)} dynamic-update-slice(bf16[2,512,4,64]{1,0,3,2:T(2,128)(2,1)} %get-tuple-element.503, bf16[1,512,4,64]{1,0,3,2:T(2,128)(2,1)} %copy.86, s32[]{:T(128)S(6)} %copy.108, s32[]{:T(128)} %constant.230.clone.1..sunk.1, s32[]{:T(128)} %constant.230.clone.1..sunk.1, s32[]{:T(128)} %constant.230.clone.1..sunk.1) | dynamic-update-slice | bytes 524292 | tf_op jit(solution)/shard_map/while/body/jit(dynamic_update_index_in_dim)/dynamic_update_slice | solution.py:211
  450.6 2.2 stack_reshape.9
  452.8 1.9 maximum_convert_fusion
  456.1 3.0 convolution_convert_fusion.6
  459.2 5.1 convolution_convert_fusion.5
  464.4 7.0 %convolution_convert_fusion.3 = bf16[1024,1024]{1,0:T(8,128)(2,1)} fusion(bf16[1024,1024]{1,0:T(8,128)(2,1)} %all-gather.16.cloned.1.call-done, f32[1024,1024]{1,0:T(8,128)} %fusion.78, f32[1024]{0:T(1024)S(1)} %reshape.375), kind=kOutput, calls=%fused_computation.89 | convolution fusion | flops 2159017984 | bytes 8392704 | tf_op jit(solution)/shard_map/dot_general | solution.py:86
  475.1 1.8 convert_element_type.168
  478.5 22.5 %all-reduce.16 = (bf16[32,16]{1,0:T(8,128)(2,1)S(1)}, bf16[64,16]{1,0:T(8,128)(2,1)S(1)}) all-reduce(bf16[32,16]{1,0:T(8,128)(2,1)S(1)} %convert_element_type.163, bf16[64,16]{1,0:T(8,128)(2,1)S(1)} %convert_element_type.169), channel_id=9, replica_groups=mesh['dp'=8,'tensor'=4] {'dp'}, use_global_device_ids=true, to_apply=%region_27.28.clone | all-reduce | flops 1536 | bytes 6144
  505.3 1.7 convert_element_type.162
  507.0 43.3 %reduce-scatter.21.cloned.1.call-done = bf16[256,1024]{1,0:T(8,128)(2,1)} async-done(((bf16[1024,1024]{1,0:T(8,128)(2,1)}), bf16[256,1024]{1,0:T(8,128)(2,1)}) %reduce-scatter.21.cloned.1.call-update) | async-done | bytes 524304 | tf_op jit(solution)/shard_map/reduce_scatter | solution.py:101
  550.3 1.6 fusion.69
  551.9 43.7 %all-reduce.14 = (f32[1024]{0:T(1024)S(1)}, f32[1024]{0:T(1024)S(1)}, f32[1024]{0:T(1024)S(1)}, f32[1024]{0:T(1024)S(1)}, f32[1024]{0:T(1024)S(1)}, /*index=5*/f32[1024]{0:T(1024)S(1)}, f32[1024]{0:T(1024)S(1)}) all-reduce(f32[1024]{0:T(1024)S(1)} %dynamic-update-slice.5, ...), channel_id=1, replica_groups=mesh['dp'=8,'tensor'=4] {'dp','tensor'}, use_global_device_ids=true, to_apply=%add.5 | all-reduce | flops 7168 | bytes 57344
  599.1 2.7 fusion.62
  (194 shorter events, 50.4 us)
Async XLA Ops:
  7.2 69.9 %all-gather.10.cloned.1.call-start = ((), (), s32[]{:S(2)}) async-start(), calls=%async_computation.9 | async-start | bytes 1769472 | tf_op jit(solution)/shard_map/all_gather | solution.py:244
  7.9 94.0 %all-gather.8.cloned.1.call-start = ((), (), s32[]{:S(2)}) async-start(), calls=%async_computation.8 | async-start | bytes 2621440 | tf_op jit(solution)/shard_map/all_gather | solution.py:53
  53.7 12.7 %copy-start.12 = (f32[1024]{0:T(1024)}, f32[1024]{0:T(1024)S(1)}, u32[]{:S(2)}) copy-start(f32[1024]{0:T(1024)S(1)} %get-tuple-element.305) | copy-start | bytes 12292
  54.9 11.5 %copy-start.14 = (f32[256]{0:T(256)}, f32[256]{0:T(256)S(1)}, u32[]{:S(2)}) copy-start(f32[256]{0:T(256)S(1)} %broadcast_multiply_fusion.5) | copy-start | bytes 3076
  56.3 10.1 %copy-start.16 = (f32[256]{0:T(256)}, f32[256]{0:T(256)S(1)}, u32[]{:S(2)}) copy-start(f32[256]{0:T(256)S(1)} %add_rsqrt_fusion.1) | copy-start | bytes 3076
  58.4 114.3 %reduce-scatter.15.cloned.1.call-start = ((), (), s32[]{:S(2)}) async-start(), calls=%async_computation.10 | async-start | bytes 2621440 | tf_op jit(solution)/shard_map/reduce_scatter | solution.py:88
  105.8 0.7 copy-start.11
  126.6 46.1 %copy-start = (bf16[256,1024]{1,0:T(8,128)(2,1)S(1)}, bf16[256,1024]{1,0:T(8,128)(2,1)}, u32[]{:S(2)}) copy-start(bf16[256,1024]{1,0:T(8,128)(2,1)} %param.19) | copy-start | bytes 1572868
  126.7 0.8 copy-start.7
  129.6 48.6 %copy-start.9 = (bf16[256,1024]{1,0:T(8,128)(2,1)S(1)}, bf16[256,1024]{1,0:T(8,128)(2,1)}, u32[]{:S(2)}) copy-start(bf16[256,1024]{1,0:T(8,128)(2,1)} %param.33) | copy-start | bytes 1572868
  129.6 75.3 %copy-start.19 = (bf16[64,2]{0,1:T(2,128)(2,1)S(1)}, bf16[64,2]{0,1:T(2,128)(2,1)}, u32[]{:S(2)}) copy-start(bf16[64,2]{0,1:T(2,128)(2,1)} %param.30) | copy-start | bytes 772
  129.7 92.6 %all-gather.14.cloned.1.call-start = ((), (), s32[]{:S(2)}) async-start(), calls=%async_computation.12 | async-start | bytes 2359296 | tf_op jit(solution)/shard_map/all_gather | solution.py:249
  130.2 118.5 %all-gather.12.cloned.1.call-start = ((), (), s32[]{:S(2)}) async-start(), calls=%async_computation.11 | async-start | bytes 2621440 | tf_op jit(solution)/shard_map/all_gather | solution.py:53
  177.6 101.3 %all-gather.16.cloned.1.call-start = ((), (), s32[]{:S(2)}) async-start(), calls=%async_computation.13 | async-start | bytes 2359296 | tf_op jit(solution)/shard_map/all_gather | solution.py:251
  178.2 158.6 %reduce-scatter.19.cloned.1.call-start = ((), (), s32[]{:S(2)}) async-start(), calls=%async_computation.15 | async-start | bytes 2621440 | tf_op jit(solution)/shard_map/reduce_scatter | solution.py:101
  178.2 23.6 %collective-permute-start = (bf16[256,1024]{1,0:T(8,128)(2,1)S(1)}, bf16[256,1024]{1,0:T(8,128)(2,1)}, u32[]{:S(2)}, u32[]{:S(2)}) collective-permute-start(bf16[256,1024]{1,0:T(8,128)(2,1)S(1)} %copy-done.9), channel_id=1, source_target_pairs={{0,1},{1,2},{2,3},{3,0},{4,5},{5,6},{6,7},{7,4},{8,9},{9,10},{10,1... | collective-permute-start | bytes 1572872 | tf_op jit(solution)/shard_map/ppermute | solution.py:67
  179.8 34.2 %collective-permute-start.2 = (bf16[256,1024]{1,0:T(8,128)(2,1)S(1)}, bf16[256,1024]{1,0:T(8,128)(2,1)}, u32[]{:S(2)}, u32[]{:S(2)}) collective-permute-start(bf16[256,1024]{1,0:T(8,128)(2,1)S(1)} %copy-done.9), channel_id=1, source_target_pairs={{1,0},{2,1},{3,2},{0,3},{5,4},{6,5},{7,6},{4,7},{9,8},{10,9},{11,1... | collective-permute-start | bytes 1572872 | tf_op jit(solution)/shard_map/ppermute | solution.py:70
  201.8 13.9 %collective-permute-start.1 = (bf16[256,1024]{1,0:T(8,128)(2,1)}, bf16[256,1024]{1,0:T(8,128)(2,1)}, u32[]{:S(2)}, u32[]{:S(2)}) collective-permute-start(bf16[256,1024]{1,0:T(8,128)(2,1)} %collective-permute-done), channel_id=1, source_target_pairs={{0,1},{1,2},{2,3},{3,0},{4,5},{5,6},{6,7},{7,4},{8,9},{9,10},{10,1... | collective-permute-start | bytes 1572872 | tf_op jit(solution)/shard_map/ppermute | solution.py:67
  278.9 10.9 %copy-start.21 = (bf16[1024,1024]{1,0:T(8,128)(2,1)S(1)}, bf16[1024,1024]{1,0:T(8,128)(2,1)}, u32[]{:S(2)}) copy-start(bf16[1024,1024]{1,0:T(8,128)(2,1)} %all-gather.14.cloned.1.call-done) | copy-start | bytes 6291460
  288.5 1.4 copy-start.24
  293.6 179.5 %reduce-scatter.29.cloned.1.call-start = ((), (), s32[]{:S(2)}) async-start(), calls=%async_computation.20 | async-start | bytes 2359296
  305.0 31.9 %copy-start.1 = (bf16[256,1024]{1,0:T(8,128)(2,1)S(1)}, bf16[256,1024]{1,0:T(8,128)(2,1)}, u32[]{:S(2)}) copy-start(bf16[256,1024]{1,0:T(8,128)(2,1)} %reduce-scatter.15.cloned.1.call-done) | copy-start | bytes 1572868
  305.0 170.1 %reduce-scatter.25.cloned.1.call-start = ((), (), s32[]{:S(2)}) async-start(), calls=%async_computation.18 | async-start | bytes 2359296 | tf_op jit(solution)/shard_map/reduce_scatter | solution.py:292
  311.1 191.4 %reduce-scatter.27.cloned.1.call-start = ((), (), s32[]{:S(2)}) async-start(), calls=%async_computation.19 | async-start | bytes 589824
  340.4 1.0 copy-start.3
  341.5 23.7 %collective-permute-start.3 = (bf16[256,1024]{1,0:T(8,128)(2,1)S(1)}, bf16[256,1024]{1,0:T(8,128)(2,1)}, u32[]{:S(2)}, u32[]{:S(2)}) collective-permute-start(bf16[256,1024]{1,0:T(8,128)(2,1)S(1)} %convert_element_type.154), channel_id=1, source_target_pairs={{0,1},{1,2},{2,3},{3,0},{4,5},{5,6},{6,7},{7,4},{8,9},{9,10},{10,1... | collective-permute-start | bytes 1572872 | tf_op jit(solution)/shard_map/ppermute | solution.py:67
  343.1 26.5 %collective-permute-start.5 = (bf16[256,1024]{1,0:T(8,128)(2,1)S(1)}, bf16[256,1024]{1,0:T(8,128)(2,1)}, u32[]{:S(2)}, u32[]{:S(2)}) collective-permute-start(bf16[256,1024]{1,0:T(8,128)(2,1)S(1)} %convert_element_type.154), channel_id=1, source_target_pairs={{1,0},{2,1},{3,2},{0,3},{5,4},{6,5},{7,6},{4,7},{9,8},{10,9},{11,1... | collective-permute-start | bytes 1572872 | tf_op jit(solution)/shard_map/ppermute | solution.py:70
  365.2 11.9 %collective-permute-start.4 = (bf16[256,1024]{1,0:T(8,128)(2,1)}, bf16[256,1024]{1,0:T(8,128)(2,1)}, u32[]{:S(2)}, u32[]{:S(2)}) collective-permute-start(bf16[256,1024]{1,0:T(8,128)(2,1)} %collective-permute-done.3), channel_id=1, source_target_pairs={{0,1},{1,2},{2,3},{3,0},{4,5},{5,6},{6,7},{7,4},{8,9},{9,10},{10,1... | collective-permute-start | bytes 1572872 | tf_op jit(solution)/shard_map/ppermute | solution.py:67
  380.1 3.7 copy-start.8
  392.1 113.1 %reduce-scatter.23.cloned.1.call-start = ((), (), s32[]{:S(2)}) async-start(), calls=%async_computation.17 | async-start | bytes 1769472 | tf_op jit(solution)/shard_map/reduce_scatter | solution.py:327
  397.3 1.3 copy-start.6
  425.6 1.3 copy-start.6
  452.8 3.3 copy-start.20
  454.7 4.5 copy-start.5
  454.8 1.3 copy-start.10
  459.2 91.1 %reduce-scatter.21.cloned.1.call-start = ((), (), s32[]{:S(2)}) async-start(), calls=%async_computation.16 | async-start | bytes 2621440 | tf_op jit(solution)/shard_map/reduce_scatter | solution.py:101
  464.3 7.2 %copy-start.23 = (u32[32]{0:T(128)S(1)}, u32[32]{0:T(128)}, u32[]{:S(2)}) copy-start(u32[32]{0:T(128)} %constant.278) | copy-start | bytes 388
  464.3 8.4 %copy-start.22 = (f32[32]{0:T(128)S(1)}, f32[32]{0:T(128)}, u32[]{:S(2)}) copy-start(f32[32]{0:T(128)} %param.32) | copy-start | bytes 388
  464.3 8.7 %copy-start.18 = (bf16[1024]{0:T(1024)(128)(2,1)S(1)}, bf16[1024]{0:T(1024)(128)(2,1)}, u32[]{:S(2)}) copy-start(bf16[1024]{0:T(1024)(128)(2,1)} %get-tuple-element.314) | copy-start | bytes 6148
  464.3 134.8 %reduce-scatter.17.cloned.1.call-start = ((), (), s32[]{:S(2)}) async-start(), calls=%async_computation.14 | async-start | bytes 2621440 | tf_op jit(solution)/shard_map/reduce_scatter | solution.py:88
  471.4 78.9 %copy-start.13 = (f32[1024]{0:T(1024)S(1)}, f32[1024]{0:T(1024)}, u32[]{:S(2)}) copy-start(f32[1024]{0:T(1024)} %copy-done.12) | copy-start | bytes 12292
  471.4 78.9 %copy-start.15 = (f32[256]{0:T(256)S(1)}, f32[256]{0:T(256)}, u32[]{:S(2)}) copy-start(f32[256]{0:T(256)} %copy-done.14) | copy-start | bytes 3076
  471.4 78.9 %copy-start.17 = (f32[256]{0:T(256)S(1)}, f32[256]{0:T(256)}, u32[]{:S(2)}) copy-start(f32[256]{0:T(256)} %copy-done.16) | copy-start | bytes 3076
  471.5 127.7 %copy-start.2 = (bf16[256,1024]{1,0:T(8,128)(2,1)S(1)}, bf16[256,1024]{1,0:T(8,128)(2,1)}, u32[]{:S(2)}) copy-start(bf16[256,1024]{1,0:T(8,128)(2,1)} %reduce-scatter.15.cloned.1.call-done) | copy-start | bytes 1572868
  471.5 127.7 %copy-start.4 = (f32[256,1024]{1,0:T(8,128)S(1)}, f32[256,1024]{1,0:T(8,128)}, u32[]{:S(2)}) copy-start(f32[256,1024]{1,0:T(8,128)} %copy-done.3) | copy-start | bytes 3145732
Sparse Core Ops, SparseCore 0:
  9.9 26.7 all-gather.9
  58.6 43.3 all-gather.7
  129.8 42.9 reduce-scatter.14
  174.5 27.7 all-gather.13
  204.3 44.4 all-gather.11
  250.5 28.3 all-gather.15
  293.7 43.1 reduce-scatter.18
  340.1 41.1 reduce-scatter.28
  384.6 41.1 reduce-scatter.24
  429.3 34.1 reduce-scatter.26
  466.7 38.4 reduce-scatter.22
  507.4 42.8 reduce-scatter.20
  552.6 43.8 reduce-scatter.16
